TPU v7x, 256 devices: a whole 4x4x8 slice. The times are simulated.
256 devices in a mesh: dp: 16 (over x, z_hi, core), expert: 16 (over y, z_lo).
Axes of the slice: x: 4, y: 4, z: 8 (z_hi: 2, z_lo: 4; z = z_hi * 4 + z_lo), core: 2. Of those that a mesh axis runs over, the one named last changes fastest.
Arguments:
- hidden: bfloat16 [16, 2048, 1792], P('expert', 'dp'), may hold values from -6 to 6
- outgrad: bfloat16 [16, 2048, 4096], P('expert', 'dp'), may hold values from -6 to 6
- row_expert: int32 [16, 2048], P('expert', 'dp'), may hold values from 0 to 1
- counts: int32 [16, 16], P('expert', 'dp'), may hold values from 1 to 128, as said below
- learner_map: int32 [256], replicated, may hold values from 0 to 255, as said below
- rollout_map: int32 [256], replicated, may hold values from 0 to 255, as said below
- master: float32 [4096, 28672], P('dp', 'expert'), may hold values from -3 to 3
- moment1: float32 [4096, 28672], P('dp', 'expert'), may hold values from -12 to 12
- moment2: float32 [4096, 28672], P('dp', 'expert'), may hold values from 1 to 1000
Outputs:
- new_master: float32 [4096, 28672], P('dp', 'expert')
- new_moment1: float32 [4096, 28672], P('dp', 'expert')
- new_moment2: float32 [4096, 28672], P('dp', 'expert')
- rollout_weights: bfloat16 [4096, 28672], P('dp', 'expert')
Inputs may be any that keep to these rules, and one draw needn't show every extreme that they name: `counts`: some device has exactly 128 live rows in every draw. `learner_map`: a permutation of the units. `rollout_map`: a permutation of the units; the 16 units at the positions of one learner device lie at positions of 16 different rollout devices, one each.
All inputs are finite; a program needn't handle non-finite values.
Results may differ from a plain program's by a relative error of at most 0.0095.
Values may be sent and summed in bfloat16 or wider, within the bound.
A program may use at most 128 MiB of HBM per device.

v0:
```python
import jax
import jax.numpy as jnp
from jax import lax
from jax.sharding import Mesh
from jax.sharding import PartitionSpec as P

FF = 14336
DP = ("dp_0", "dp_1", "dp_2")
beta_one = 0.9
beta_two = 0.95
learn_rate = 0.01
decay_rate = 0.1
epsilon = 1e-08
step_count = 100.0


def split_up(value, dim, devices):
    before, after = (value.shape[:dim], value.shape[dim + 1 :])
    return jnp.moveaxis(value.reshape(*before, devices, -1, *after), dim, 0)


def joined_along(blocks, dim):
    blocks = jnp.moveaxis(blocks, 0, dim)
    lengths = blocks.shape
    return blocks.reshape(*lengths[:dim], lengths[dim] * lengths[dim + 1], *lengths[dim + 2 :])


def exchange_in_order(blocks, axes, turns):
    inside = blocks.shape[1:]
    out = blocks.reshape(*(lax.axis_size(a) for a in axes), *inside)
    for k in turns:
        out = lax.all_to_all(out, axes[k], k, k, tiled=True)
    return out.reshape(-1, *inside)


def core_and_chips(value, groups, turns, split_dim, concat_dim):
    devices = lax.axis_size(groups[0]) * lax.axis_size(groups[1])
    blocks = split_up(value, split_dim, devices)
    return joined_along(exchange_in_order(blocks, groups, turns), concat_dim)


def on_device(
    hidden, outgrad, row_expert, counts, learner_map, rollout_map, master, moment1, moment2
):
    hidden = hidden[0]
    outgrad = outgrad[0]
    groups = lax.axis_size("expert")
    own_index = lax.axis_index("expert")
    block_width = hidden.shape[1] // groups
    per_expert = FF // block_width
    tok_rows = hidden.shape[0]
    width_share = master.shape[0]
    slot_units = lax.dynamic_slice_in_dim(learner_map, own_index * groups, groups)
    slot_expert = slot_units // per_expert
    live_rows = jnp.arange(tok_rows, dtype=jnp.int32) < counts[0, 0]
    kept = live_rows[:, None] & (row_expert[0][:, None] == slot_expert[None, :])
    kept_cols = jnp.repeat(kept, block_width, axis=1)
    masked = jnp.where(kept_cols, hidden, jnp.zeros((), jnp.bfloat16))
    contract = (((0,), (0,)), ((), ()))
    sliced = core_and_chips(outgrad, (("dp_0", "dp_1"), "dp_2"), (1, 0), 1, 0)
    gradient = lax.dot_general(
        sliced,
        lax.all_gather(masked, DP, axis=0, tiled=True),
        contract,
        preferred_element_type=jnp.float32,
    )
    new_moment1 = beta_one * moment1 + (1.0 - beta_one) * gradient
    new_moment2 = beta_two * moment2 + (1.0 - beta_two) * gradient * gradient
    bias_one = 1.0 - beta_one**step_count
    bias_two = 1.0 - beta_two**step_count
    update = new_moment1 / bias_one / (jnp.sqrt(new_moment2 / bias_two) + epsilon)
    new_master = master - learn_rate * (update + decay_rate * master)
    inverse_roll = jnp.argsort(rollout_map)
    inverse_learn = jnp.argsort(learner_map)
    target = inverse_roll[slot_units] // groups
    send_order = jnp.argsort(target)
    rounded = new_master.astype(jnp.bfloat16).reshape(width_share, groups, block_width)
    outgoing = jnp.take(rounded, send_order, axis=1).reshape(width_share, groups * block_width)
    incoming = lax.all_to_all(outgoing, "expert", split_axis=1, concat_axis=1, tiled=True).reshape(
        width_share, groups, block_width
    )
    wanted = lax.dynamic_slice_in_dim(rollout_map, own_index * groups, groups)
    source = inverse_learn[wanted] // groups
    rollout_weights = jnp.take(incoming, source, axis=1).reshape(width_share, groups * block_width)
    return (new_master, new_moment1, new_moment2, rollout_weights)


def solution(mesh):
    finer = Mesh(
        mesh.devices.reshape(4, 2, 2, mesh.shape["expert"]), ("dp_0", "dp_1", "dp_2", "expert")
    )
    return jax.shard_map(
        on_device,
        mesh=finer,
        in_specs=(
            P("expert", DP, None),
            P("expert", DP, None),
            P("expert", DP),
            P("expert", DP),
            P(),
            P(),
            P(DP, "expert"),
            P(DP, "expert"),
            P(DP, "expert"),
        ),
        out_specs=(P(DP, "expert"), P(DP, "expert"), P(DP, "expert"), P(DP, "expert")),
        check_vma=False,
    )
```

profile of v0, /device:TPU:1, one launch (start us, length us, event | category | flops | bytes accessed | tf_op | source)
XLA Modules:
  0.0 188.4 jit_solution(5097774377998562409)
XLA Ops:
  7.2 0.0 copy-start.2
  7.2 0.0 all-gather.2.cloned.1.call-start
  8.0 1.3 copy.53
  9.2 0.8 compare_select_fusion.3
  10.0 0.7 compare_and_fusion
  10.8 0.8 bitcast_select_fusion
  11.6 0.0 all-gather.2.cloned.1.call-update
  11.6 0.0 copy-done.2
  11.6 0.7 copy.54
  12.3 0.5 copy.56
  12.8 7.4 %all_to_all.16 = bf16[8,2,128,256]{3,2,0,1:T(8,128)(2,1)S(1)} all-to-all(bf16[8,2,128,256]{3,2,0,1:T(8,128)(2,1)S(1)} %copy.56), channel_id=1, replica_groups=mesh['dp_0'=4,'dp_1'=2,'dp_2'=2,'expert'=16] {'dp_2'}, dimensions={1} | all-to-all | bytes 2097152 | tf_op jit(solution)/shard_map/all_to_all | solution.py:32
  20.2 0.0 copy-start
  20.2 1.0 copy.57
  21.3 8.9 %all-to-all-start.1 = ((bf16[8,2,128,256]{3,2,1,0:T(8,128)(2,1)}), bf16[8,2,128,256]{3,2,1,0:T(8,128)(2,1)S(1)}, u32[]{:S(2)}, u32[]{:S(2)}) async-start(bf16[8,2,128,256]{3,2,1,0:T(8,128)(2,1)} %copy.57), calls=%async_computation.1 | async-start | bytes 2097152 | tf_op jit(solution)/shard_map/all_to_all | solution.py:32
  30.2 0.0 copy-done
  30.2 1.7 copy.52
  31.9 0.0 copy-start.1
  31.9 2.9 %copy.58 = f32[256,1792]{0,1:T(8,128)} copy(f32[256,1792]{1,0:T(8,128)} %param.19) | data formatting | bytes 3670016 | tf_op args[8]
  34.7 0.0 copy-done.1
  34.7 0.0 copy-start.4
  34.7 1.7 copy.60
  36.4 0.0 copy-done.4
  36.4 3.1 %sort.48 = (s32[256]{0:T(256)}, s32[256]{0:T(256)S(1)}) sort(s32[256]{0:T(256)S(1)} %copy-done.4, s32[256]{0:T(256)S(1)} %iota.17), dimensions={0}, to_apply=%region_0.1 | sort | flops 2048 | bytes 4096 | tf_op jit(solution)/shard_map/jit(argsort)/sort | solution.py:73
  39.6 0.7 gather_fusion
  40.2 1.2 sort.49
  41.5 19.8 %all-to-all-done.1 = bf16[8,2,128,256]{3,2,1,0:T(8,128)(2,1)S(1)} async-done(((bf16[8,2,128,256]{3,2,1,0:T(8,128)(2,1)}), bf16[8,2,128,256]{3,2,1,0:T(8,128)(2,1)S(1)}, u32[]{:S(2)}, u32[]{:S(2)}) %all-to-all-start.1) | async-done | bytes 1048608 | tf_op jit(solution)/shard_map/all_to_all | solution.py:32
  61.3 0.0 copy-start.3
  61.3 76.0 %all-gather.2.cloned.1.call-done = bf16[2048,1792]{0,1:T(8,128)(2,1)} async-done(((bf16[128,1792]{0,1:T(8,128)(2,1)}), bf16[2048,1792]{0,1:T(8,128)(2,1)}) %all-gather.2.cloned.1.call-update) | async-done | bytes 7340048 | tf_op jit(solution)/shard_map/all_gather | solution.py:63
  137.3 0.0 copy-done.3
  137.3 10.6 %fusion.1 = (bf16[256,1792]{0,1:T(8,128)(2,1)}, f32[256,1792]{0,1:T(8,128)}, f32[256,1792]{0,1:T(8,128)}, f32[256,1792]{0,1:T(8,128)S(1)}) fusion(f32[256,1792]{0,1:T(8,128)} %copy.60, f32[256,1792]{0,1:T(8,128)} %copy.52, f32[256,1792]{0,1:T(8,128)} %copy.58, bf16[2048,1792]{0,1:T(8,128)(2,1)} %all-gather.2.cloned.1.call-done, bf16[2048,256]{1,0:T(8,128)(2,1)} %bitcast.26), kind=kOutput, calls=%fused_computation.36 | convolution fusion | flops 1886388224 | bytes 20316160 | tf_op jit(solution)/shard_map/dot_general | solution.py:61
  147.9 1.8 gather_fusion.2
  149.7 0.0 copy-start.5
  149.7 1.1 select_bitcast_fusion
  150.8 4.3 %all-to-all-start.2 = ((bf16[256,16,112]{0,2,1:T(8,128)(2,1)}), bf16[256,16,112]{0,2,1:T(8,128)(2,1)S(1)}, u32[]{:S(2)}, u32[]{:S(2)}) async-start(bf16[256,16,112]{0,2,1:T(8,128)(2,1)} %select_bitcast_fusion), calls=%async_computation.2 | async-start | bytes 1835008 | tf_op jit(solution)/shard_map/all_to_all | solution.py:79
  155.1 0.0 copy-done.5
  155.1 3.2 %sort.50 = (s32[256]{0:T(256)}, s32[256]{0:T(256)S(1)}) sort(s32[256]{0:T(256)S(1)} %copy-done.5, s32[256]{0:T(256)S(1)} %iota.19), dimensions={0}, to_apply=%region_2.4 | sort | flops 2048 | bytes 4096 | tf_op jit(solution)/shard_map/jit(argsort)/sort | solution.py:74
  158.3 0.7 gather_fusion.1
  159.0 2.7 %copy.61 = f32[256,1792]{1,0:T(8,128)} copy(f32[256,1792]{0,1:T(8,128)} %get-tuple-element.34) | data formatting | bytes 3670016
  161.7 2.7 %copy.62 = f32[256,1792]{1,0:T(8,128)} copy(f32[256,1792]{0,1:T(8,128)} %get-tuple-element.35) | data formatting | bytes 3670016
  164.5 1.7 copy.63
  166.1 13.3 %all-to-all-done.2 = bf16[256,16,112]{0,2,1:T(8,128)(2,1)S(1)} async-done(((bf16[256,16,112]{0,2,1:T(8,128)(2,1)}), bf16[256,16,112]{0,2,1:T(8,128)(2,1)S(1)}, u32[]{:S(2)}, u32[]{:S(2)}) %all-to-all-start.2) | async-done | bytes 917536 | tf_op jit(solution)/shard_map/all_to_all | solution.py:79
  179.4 0.6 gather_fusion.3
  180.0 0.1 broadcast_select_fusion
  180.2 1.4 copy.64
  (12 shorter events, 0.1 us)
Async XLA Ops:
  7.2 4.4 %copy-start.2 = (bf16[1,128,4096]{2,1,0:T(8,128)(2,1)S(1)}, bf16[1,128,4096]{2,1,0:T(8,128)(2,1)}, u32[]{:S(2)}) copy-start(bf16[1,128,4096]{2,1,0:T(8,128)(2,1)} %param.12) | copy-start | bytes 3145732
  7.2 130.2 %all-gather.2.cloned.1.call-start = ((), (), s32[]{:S(2)}) async-start(), calls=%async_computation.3 | async-start | bytes 7798784 | tf_op jit(solution)/shard_map/all_gather | solution.py:63
  20.2 10.0 %copy-start = (f32[256,1792]{1,0:T(8,128)S(1)}, f32[256,1792]{1,0:T(8,128)}, u32[]{:S(2)}) copy-start(f32[256,1792]{1,0:T(8,128)} %param.18) | copy-start | bytes 5505028
  21.3 40.1 %all-to-all-start.1 = ((bf16[8,2,128,256]{3,2,1,0:T(8,128)(2,1)}), bf16[8,2,128,256]{3,2,1,0:T(8,128)(2,1)S(1)}, u32[]{:S(2)}, u32[]{:S(2)}) async-start(bf16[8,2,128,256]{3,2,1,0:T(8,128)(2,1)} %copy.57), calls=%async_computation.1 | async-start | bytes 2097152 | tf_op jit(solution)/shard_map/all_to_all | solution.py:32
  31.9 2.9 %copy-start.1 = (f32[256,1792]{1,0:T(8,128)S(1)}, f32[256,1792]{1,0:T(8,128)}, u32[]{:S(2)}) copy-start(f32[256,1792]{1,0:T(8,128)} %param.17) | copy-start | bytes 5505028
  34.7 1.7 copy-start.4
  61.3 76.0 %copy-start.3 = (bf16[8,2,128,256]{3,2,1,0:T(8,128)(2,1)}, bf16[8,2,128,256]{3,2,1,0:T(8,128)(2,1)S(1)}, u32[]{:S(2)}) copy-start(bf16[8,2,128,256]{3,2,1,0:T(8,128)(2,1)S(1)} %all-to-all-done.1) | copy-start | bytes 3145732
  149.7 5.4 %copy-start.5 = (s32[256]{0:T(256)S(1)}, s32[256]{0:T(256)}, u32[]{:S(2)}) copy-start(s32[256]{0:T(256)} %param.15) | copy-start | bytes 3076
  150.8 28.6 %all-to-all-start.2 = ((bf16[256,16,112]{0,2,1:T(8,128)(2,1)}), bf16[256,16,112]{0,2,1:T(8,128)(2,1)S(1)}, u32[]{:S(2)}, u32[]{:S(2)}) async-start(bf16[256,16,112]{0,2,1:T(8,128)(2,1)} %select_bitcast_fusion), calls=%async_computation.2 | async-start | bytes 1835008 | tf_op jit(solution)/shard_map/all_to_all | solution.py:79
Sparse Core Ops, SparseCore 0:
  11.7 125.5 all-gather.1
where the time goes:
time: 189 us; the launch traced here: 188 us
  waiting for transfers between devices  109 us (58%)
  local copies, waits for them, and re-layouts  22 us (12%)
  between operations  14.9 us (8%)
  starting transfers between devices  13.3 us (7%)
  other arithmetic  11.1 us (6%)
  matrix products  10.6 us (6%)
  blocking collectives  7.4 us (4%)
    all_gather x1, waiting for transfers between devices, on_device(): lax.all_gather(masked, DP, axis=0, tiled=True)  76 us
    all_to_all x1, waiting for transfers between devices, exchange_in_order(): out = lax.all_to_all(out, axes[k], k, k, tiled=True)  19.8 us
    unnamed x21, local copies, waits for them, and re-layouts  16.7 us
    all_to_all x1, waiting for transfers between devices, on_device(): lax.all_to_all(outgoing, 'expert', split_axis=1, concat_axis=1, tiled=True)  13.3 us
    dot_general x1, matrix products, on_device(): lax.dot_general(sliced, lax.all_gather(masked, DP, axis=0, tiled=True), c...  10.6 us
    all_to_all x1, starting transfers between devices, exchange_in_order(): out = lax.all_to_all(out, axes[k], k, k, tiled=True)  8.94 us
    all_to_all x1, blocking collectives, exchange_in_order(): out = lax.all_to_all(out, axes[k], k, k, tiled=True)  7.4 us
    all_to_all x1, starting transfers between devices, on_device(): lax.all_to_all(outgoing, 'expert', split_axis=1, concat_axis=1, tiled=True)  4.34 us
  transfers between devices with their start and end apart: 3, of which 3 were waited for; matrix products, arithmetic and copies ran while one was open for 13% of the time, Pallas kernels for 0%

commit v1 on v0

--- a/solution.py
+++ b/solution.py
@@ -60,7 +60,7 @@
     sliced = core_and_chips(outgrad, (("dp_0", "dp_1"), "dp_2"), (1, 0), 1, 0)
     gradient = lax.dot_general(
         sliced,
-        lax.all_gather(masked, DP, axis=0, tiled=True),
+        jnp.concatenate(lax.all_to_all(jnp.stack([masked] * lax.axis_size(DP)), DP, 0, 0), axis=0),
         contract,
         preferred_element_type=jnp.float32,
     )

time: 189 us -> 270 us (1.43)
  starting transfers between devices: 13.3 us -> 106 us
  between operations: 14.9 us -> 1.43 us
  local copies, waits for them, and re-layouts: 22 us -> 25.9 us
    all_to_all x1, starting transfers between devices: 4.34 us -> 86.3 us  [on_device(): lax.all_to_all(outgoing, 'expert', split_axis=1, concat_axis=1, tiled=True)]
    all_gather x1 -> x0, waiting for transfers between devices: 76 us -> none  [on_device(): lax.all_gather(masked, DP, axis=0, tiled=True)]
    all_to_all x0 -> x1, waiting for transfers between devices: none -> 75.9 us  [on_device(): lax.all_to_all(jnp.stack([masked] * lax.axis_size(DP)), DP, 0, 0)]
    all_to_all x0 -> x1, starting transfers between devices: none -> 10.4 us  [on_device(): lax.all_to_all(jnp.stack([masked] * lax.axis_size(DP)), DP, 0, 0)]
    another operation x0 -> x2, local copies, waits for them, and re-layouts: none -> 3.96 us  [on_device(): jnp.stack([masked] * lax.axis_size(DP))]
    unnamed x21 -> x23, local copies, waits for them, and re-layouts: 16.7 us -> 16.6 us
  transfers between devices with their start and end apart: 3 -> 3, of which waited for: 3 -> 3; matrix products, arithmetic and copies ran while one was open for 13% -> 9% of each run, Pallas kernels for 0% -> 0%
where the time goes in v1:
time: 270 us; the launch traced here: 269 us
  waiting for transfers between devices  109 us (40%)
  starting transfers between devices  106 us (39%)
  local copies, waits for them, and re-layouts  25.9 us (10%)
  matrix products  10.5 us (4%)
  other arithmetic  9.08 us (3%)
  blocking collectives  7.4 us (3%)
    all_to_all x1, starting transfers between devices, on_device(): lax.all_to_all(outgoing, 'expert', split_axis=1, concat_axis=1, tiled=True)  86.3 us
    all_to_all x1, waiting for transfers between devices, on_device(): lax.all_to_all(jnp.stack([masked] * lax.axis_size(DP)), DP, 0, 0)  75.9 us
    all_to_all x1, waiting for transfers between devices, exchange_in_order(): out = lax.all_to_all(out, axes[k], k, k, tiled=True)  20 us
    unnamed x23, local copies, waits for them, and re-layouts  16.6 us
    all_to_all x1, waiting for transfers between devices, on_device(): lax.all_to_all(outgoing, 'expert', split_axis=1, concat_axis=1, tiled=True)  13.2 us
    dot_general x1, matrix products, on_device(): lax.dot_general(sliced, jnp.concatenate(lax.all_to_all(jnp.stack([masked]...  10.5 us
    all_to_all x1, starting transfers between devices, on_device(): lax.all_to_all(jnp.stack([masked] * lax.axis_size(DP)), DP, 0, 0)  10.4 us
    all_to_all x1, starting transfers between devices, exchange_in_order(): out = lax.all_to_all(out, axes[k], k, k, tiled=True)  9.07 us
  transfers between devices with their start and end apart: 3, of which 3 were waited for; matrix products, arithmetic and copies ran while one was open for 9% of the time, Pallas kernels for 0%

profile of v1, /device:TPU:1, one launch (start us, length us, event | category | flops | bytes accessed | tf_op | source)
XLA Modules:
  0.0 269.2 jit_solution(223900592269281121)
XLA Ops:
  0.6 1.6 copy.58
  2.3 0.5 copy.60
  2.8 7.4 %all_to_all.21 = bf16[8,2,128,256]{3,2,0,1:T(8,128)(2,1)S(1)} all-to-all(bf16[8,2,128,256]{3,2,0,1:T(8,128)(2,1)S(1)} %copy.60), channel_id=1, replica_groups=mesh['dp_0'=4,'dp_1'=2,'dp_2'=2,'expert'=16] {'dp_2'}, dimensions={1} | all-to-all | bytes 2097152 | tf_op jit(solution)/shard_map/all_to_all | solution.py:32
  10.2 0.0 copy-start.3
  10.2 1.0 copy.61
  11.2 0.0 copy-start.4
  11.2 0.0 copy-start.5
  11.2 0.0 copy-start.6
  11.2 9.1 %all-to-all-start.2 = ((bf16[8,2,128,256]{3,2,1,0:T(8,128)(2,1)}), bf16[8,2,128,256]{3,2,1,0:T(8,128)(2,1)S(1)}, u32[]{:S(2)}, u32[]{:S(2)}) async-start(bf16[8,2,128,256]{3,2,1,0:T(8,128)(2,1)} %copy.61), calls=%async_computation.2 | async-start | bytes 2097152 | tf_op jit(solution)/shard_map/all_to_all | solution.py:32
  21.0 0.0 copy-done.3
  21.0 0.3 copy.56
  21.2 0.0 copy-done.4
  21.3 0.0 copy-done.5
  21.3 0.1 compare_select_fusion.3
  21.4 0.0 copy-done.6
  21.4 0.1 compare_and_fusion
  21.5 0.2 copy.57
  21.7 20.0 %all-to-all-done.2 = bf16[8,2,128,256]{3,2,1,0:T(8,128)(2,1)S(1)} async-done(((bf16[8,2,128,256]{3,2,1,0:T(8,128)(2,1)}), bf16[8,2,128,256]{3,2,1,0:T(8,128)(2,1)S(1)}, u32[]{:S(2)}, u32[]{:S(2)}) %all-to-all-start.2) | async-done | bytes 1048608 | tf_op jit(solution)/shard_map/all_to_all | solution.py:32
  41.7 0.0 copy-start.2
  41.7 3.7 %stack.5 = bf16[16,128,1792]{2,1,0:T(8,128)(2,1)} broadcast(bf16[128,1792]{1,0:T(8,128)(2,1)S(1)} %copy.57), dimensions={1,2} | broadcast | bytes 7798784 | tf_op jit(solution)/shard_map/stack | solution.py:63
  45.5 0.0 copy-done.2
  45.5 0.0 copy-start
  45.5 10.4 %all-to-all-start = ((bf16[16,128,1792]{2,1,0:T(8,128)(2,1)}), bf16[16,128,1792]{2,1,0:T(8,128)(2,1)}, u32[]{:S(2)}, u32[]{:S(2)}) async-start(bf16[16,128,1792]{2,1,0:T(8,128)(2,1)} %stack.5), calls=%async_computation | async-start | bytes 14680064 | tf_op jit(solution)/shard_map/all_to_all | solution.py:63
  55.9 0.0 copy-done
  55.9 1.7 copy.55
  57.6 0.0 copy-start.1
  57.6 2.9 %copy.62 = f32[256,1792]{0,1:T(8,128)} copy(f32[256,1792]{1,0:T(8,128)} %param.19) | data formatting | bytes 3670016 | tf_op args[8]
  60.4 0.0 copy-done.1
  60.4 1.7 copy.64
  62.1 3.2 %sort.48 = (s32[256]{0:T(256)}, s32[256]{0:T(256)S(1)}) sort(s32[256]{0:T(256)S(1)} %copy-done.4, s32[256]{0:T(256)S(1)} %iota.17), dimensions={0}, to_apply=%region_0.1 | sort | flops 2048 | bytes 4096 | tf_op jit(solution)/shard_map/jit(argsort)/sort | solution.py:73
  65.3 0.7 gather_fusion
  66.0 1.2 sort.49
  67.3 75.9 %all-to-all-done = bf16[16,128,1792]{2,1,0:T(8,128)(2,1)} async-done(((bf16[16,128,1792]{2,1,0:T(8,128)(2,1)}), bf16[16,128,1792]{2,1,0:T(8,128)(2,1)}, u32[]{:S(2)}, u32[]{:S(2)}) %all-to-all-start) | async-done | bytes 7340064 | tf_op jit(solution)/shard_map/all_to_all | solution.py:63
  143.1 10.5 %fusion.1 = (bf16[256,1792]{0,1:T(8,128)(2,1)}, f32[256,1792]{0,1:T(8,128)}, f32[256,1792]{0,1:T(8,128)}, f32[256,1792]{0,1:T(8,128)S(1)}) fusion(f32[256,1792]{0,1:T(8,128)} %copy.64, f32[256,1792]{0,1:T(8,128)} %copy.55, f32[256,1792]{0,1:T(8,128)} %copy.62, bf16[2048,1792]{1,0:T(8,128)(2,1)} %bitcast.4, bf16[2048,256]{1,0:T(8,128)(2,1)} %bitcast.27), kind=kOutput, calls=%fused_computation.36 | convolution fusion | flops 1886388224 | bytes 20316160 | tf_op jit(solution)/shard_map/dot_general | solution.py:61
  153.6 1.8 gather_fusion.2
  155.4 1.1 select_bitcast_fusion
  156.5 86.3 %all-to-all-start.3 = ((bf16[256,16,112]{0,2,1:T(8,128)(2,1)}), bf16[256,16,112]{0,2,1:T(8,128)(2,1)S(1)}, u32[]{:S(2)}, u32[]{:S(2)}) async-start(bf16[256,16,112]{0,2,1:T(8,128)(2,1)} %select_bitcast_fusion), calls=%async_computation.3 | async-start | bytes 1835008 | tf_op jit(solution)/shard_map/all_to_all | solution.py:79
  242.9 3.2 %sort.50 = (s32[256]{0:T(256)}, s32[256]{0:T(256)S(1)}) sort(s32[256]{0:T(256)S(1)} %copy-done.5, s32[256]{0:T(256)S(1)} %iota.19), dimensions={0}, to_apply=%region_2.4 | sort | flops 2048 | bytes 4096 | tf_op jit(solution)/shard_map/jit(argsort)/sort | solution.py:74
  246.0 0.7 gather_fusion.1
  246.7 2.7 %copy.65 = f32[256,1792]{1,0:T(8,128)} copy(f32[256,1792]{0,1:T(8,128)} %get-tuple-element.34) | data formatting | bytes 3670016
  249.5 2.7 %copy.66 = f32[256,1792]{1,0:T(8,128)} copy(f32[256,1792]{0,1:T(8,128)} %get-tuple-element.35) | data formatting | bytes 3670016
  252.2 1.7 copy.67
  253.9 13.2 %all-to-all-done.3 = bf16[256,16,112]{0,2,1:T(8,128)(2,1)S(1)} async-done(((bf16[256,16,112]{0,2,1:T(8,128)(2,1)}), bf16[256,16,112]{0,2,1:T(8,128)(2,1)S(1)}, u32[]{:S(2)}, u32[]{:S(2)}) %all-to-all-start.3) | async-done | bytes 917536 | tf_op jit(solution)/shard_map/all_to_all | solution.py:79
  267.1 0.6 gather_fusion.3
  267.7 0.1 broadcast_select_fusion
  267.9 1.4 copy.68
  (13 shorter events, 0.1 us)
Async XLA Ops:
  10.2 10.8 %copy-start.3 = (bf16[1,128,1792]{2,1,0:T(8,128)(2,1)S(1)}, bf16[1,128,1792]{2,1,0:T(8,128)(2,1)}, u32[]{:S(2)}) copy-start(bf16[1,128,1792]{2,1,0:T(8,128)(2,1)} %param.11) | copy-start | bytes 1376260
  11.2 10.0 %copy-start.4 = (s32[256]{0:T(256)S(1)}, s32[256]{0:T(256)}, u32[]{:S(2)}) copy-start(s32[256]{0:T(256)} %param.16) | copy-start | bytes 3076
  11.2 10.0 %copy-start.5 = (s32[256]{0:T(256)S(1)}, s32[256]{0:T(256)}, u32[]{:S(2)}) copy-start(s32[256]{0:T(256)} %param.15) | copy-start | bytes 3076
  11.2 10.1 %copy-start.6 = (s32[1,128]{1,0:T(1,128)S(1)}, s32[1,128]{1,0:T(1,128)}, u32[]{:S(2)}) copy-start(s32[1,128]{1,0:T(1,128)} %param.13) | copy-start | bytes 1540
  11.2 30.5 %all-to-all-start.2 = ((bf16[8,2,128,256]{3,2,1,0:T(8,128)(2,1)}), bf16[8,2,128,256]{3,2,1,0:T(8,128)(2,1)S(1)}, u32[]{:S(2)}, u32[]{:S(2)}) async-start(bf16[8,2,128,256]{3,2,1,0:T(8,128)(2,1)} %copy.61), calls=%async_computation.2 | async-start | bytes 2097152 | tf_op jit(solution)/shard_map/all_to_all | solution.py:32
  41.7 3.8 %copy-start.2 = (bf16[8,2,128,256]{3,2,1,0:T(8,128)(2,1)}, bf16[8,2,128,256]{3,2,1,0:T(8,128)(2,1)S(1)}, u32[]{:S(2)}) copy-start(bf16[8,2,128,256]{3,2,1,0:T(8,128)(2,1)S(1)} %all-to-all-done.2) | copy-start | bytes 3145732
  45.5 10.4 %copy-start = (f32[256,1792]{1,0:T(8,128)S(1)}, f32[256,1792]{1,0:T(8,128)}, u32[]{:S(2)}) copy-start(f32[256,1792]{1,0:T(8,128)} %param.18) | copy-start | bytes 5505028
  45.5 97.7 %all-to-all-start = ((bf16[16,128,1792]{2,1,0:T(8,128)(2,1)}), bf16[16,128,1792]{2,1,0:T(8,128)(2,1)}, u32[]{:S(2)}, u32[]{:S(2)}) async-start(bf16[16,128,1792]{2,1,0:T(8,128)(2,1)} %stack.5), calls=%async_computation | async-start | bytes 14680064 | tf_op jit(solution)/shard_map/all_to_all | solution.py:63
  57.6 2.9 %copy-start.1 = (f32[256,1792]{1,0:T(8,128)S(1)}, f32[256,1792]{1,0:T(8,128)}, u32[]{:S(2)}) copy-start(f32[256,1792]{1,0:T(8,128)} %param.17) | copy-start | bytes 5505028
  156.5 110.6 %all-to-all-start.3 = ((bf16[256,16,112]{0,2,1:T(8,128)(2,1)}), bf16[256,16,112]{0,2,1:T(8,128)(2,1)S(1)}, u32[]{:S(2)}, u32[]{:S(2)}) async-start(bf16[256,16,112]{0,2,1:T(8,128)(2,1)} %select_bitcast_fusion), calls=%async_computation.3 | async-start | bytes 1835008 | tf_op jit(solution)/shard_map/all_to_all | solution.py:79
